TPU v7x, 8 devices: a whole 2x2x1 slice. The times are simulated.
8 devices in a mesh: dp: 1 (over z), ep: 8 (over y, x, core).
Axes of the slice: x: 2, y: 2, z: 1, core: 2. Of those that a mesh axis runs over, the one named last changes fastest.
Arguments:
- x_in: bfloat16 [384, 2048], P(('dp', 'ep'))
- topk_idx: int32 [384, 6], P(('dp', 'ep'))
- topk_w: float32 [384, 6], P(('dp', 'ep'))
- w_up: bfloat16 [64, 2048, 1408], P('ep')
- w_down: bfloat16 [64, 1408, 2048], P('ep')
Outputs:
- output: bfloat16 [384, 2048], P(('dp', 'ep'))
All inputs are finite; a program needn't handle non-finite values.
Results may differ from a plain program's by a relative error of at most 0.001.
Values are sent between devices in bfloat16 or wider.
A program may use at most 1 GiB of HBM per device.

v0:
```python
import jax
import jax.numpy as jnp
from jax import lax
from jax.sharding import PartitionSpec as P


def slot_layout(expert_ids, num_experts, slot_cap):
    flat_ids = expert_ids.reshape(-1)
    expert_hits = (flat_ids[:, None] == jnp.arange(num_experts, dtype=jnp.int32)[None, :]).astype(jnp.int32)
    earlier = jnp.cumsum(expert_hits, axis=0) - expert_hits
    return flat_ids * slot_cap + jnp.sum(earlier * expert_hits, axis=1)


def solution(mesh):
    group = mesh.shape['ep']
    token_spec = P(('dp', 'ep'), None)
    expert_spec = P('ep', None, None)

    def local_layer(x_loc, ids_loc, gates_loc, w_up, w_down):
        tok_n, top_n = ids_loc.shape
        model_dim = x_loc.shape[1]
        local_experts = w_up.shape[0]
        num_experts = local_experts * group
        slot_cap = tok_n // 2
        slot_ids = slot_layout(ids_loc, num_experts, slot_cap)
        slot_range = jnp.arange(num_experts * slot_cap, dtype=jnp.int32)
        placed = jnp.any(slot_ids.reshape(tok_n, top_n, 1) == slot_range, axis=1).astype(jnp.bfloat16)
        send_rows = jnp.einsum('ts,tm->sm', placed, x_loc, preferred_element_type=jnp.float32).astype(jnp.bfloat16)
        send_rows = send_rows.reshape(group, local_experts, slot_cap, model_dim)
        recv_rows = lax.all_to_all(send_rows, 'ep', 0, 2, tiled=True)
        recv_rows = recv_rows.reshape(local_experts, group * slot_cap, model_dim)
        hidden = jnp.einsum('ecm,emf->ecf', recv_rows, w_up, preferred_element_type=jnp.float32)
        hidden = jax.nn.gelu(hidden, approximate=True).astype(jnp.bfloat16)
        expert_out = jnp.einsum('ecf,efm->ecm', hidden, w_down, preferred_element_type=jnp.float32).astype(jnp.bfloat16)
        expert_out = expert_out.reshape(1, local_experts, group * slot_cap, model_dim)
        back_rows = lax.all_to_all(expert_out, 'ep', 2, 0, tiled=True)
        back_rows = back_rows.reshape(num_experts * slot_cap, model_dim)
        picked = jnp.take(back_rows, slot_ids, axis=0).reshape(tok_n, top_n, model_dim)
        mixed = jnp.sum(gates_loc[:, :, None] * picked.astype(jnp.float32), axis=1)
        return mixed.astype(jnp.bfloat16)

    return jax.shard_map(local_layer, mesh=mesh, in_specs=(token_spec, token_spec, token_spec, expert_spec, expert_spec), out_specs=token_spec, check_vma=False)
```

profile of v0, /device:TPU:0, one launch (start us, length us, event | category | flops | bytes accessed | tf_op | source)
XLA Modules:
  0.0 227.3 jit_solution(11637749709735819830)
XLA Ops:
  0.0 0.0 copy-start
  0.0 0.8 copy.36
  0.8 0.1 reshape.79
  1.0 0.9 reduce-window.6
  1.9 0.2 slice_reduce_fusion
  2.2 0.1 bitcast_bitcast_fusion
  2.3 0.1 reduce_sum.23
  2.4 0.1 copy.39
  2.5 0.7 compare_and_fusion
  3.2 0.4 fusion.13
  3.6 0.0 copy-done
  3.6 1.8 convolution_convert_fusion
  5.4 75.6 %all_to_all.30 = bf16[8,8,24,2048]{3,2,1,0:T(8,128)(2,1)S(1)} all-to-all(bf16[8,8,24,2048]{3,2,1,0:T(8,128)(2,1)S(1)} %bitcast.38), channel_id=1, replica_groups=mesh['dp'=1,'ep'=8] {'ep'}, dimensions={0} | all-to-all | bytes 12582912 | tf_op jit(solution)/shard_map/all_to_all | solution.py:30
  81.1 3.2 %copy.41 = bf16[1,8,8,24,2048]{4,3,2,1,0:T(8,128)(2,1)} copy(bf16[1,8,8,24,2048]{4,3,1,2,0:T(8,128)(2,1)S(1)} %bitcast.40) | data formatting | bytes 12582912 | tf_op jit(solution)/shard_map/all_to_all | solution.py:30
  84.3 22.3 %fusion.39 = bf16[8,192,1408]{2,1,0:T(8,128)(2,1)} fusion(bf16[8,192,2048]{2,1,0:T(8,128)(2,1)} %bitcast.41, bf16[8,2048,1408]{2,1,0:T(8,128)(2,1)} %param.8), kind=kOutput, calls=%fused_computation.9.clone.clone.1 | convolution fusion | flops 8877834240 | bytes 56754176 | tf_op jit(solution)/shard_map/ecm,emf->ecf/dot_general | solution.py:32
  106.6 18.7 %convert_bitcast_fusion = bf16[1,8,192,2048]{3,2,1,0:T(8,128)(2,1)S(1)} fusion(bf16[8,1408,2048]{2,1,0:T(8,128)(2,1)} %param.9, bf16[8,192,1408]{2,1,0:T(8,128)(2,1)} %fusion.39), kind=kOutput, calls=%fused_computation.11 | convolution fusion | flops 8861515776 | bytes 56754176 | tf_op jit(solution)/shard_map/ecf,efm->ecm/dot_general | solution.py:34
  125.3 6.1 %copy.42 = bf16[1,8,192,2048]{3,1,0,2:T(8,128)(2,1)} copy(bf16[1,8,192,2048]{3,2,1,0:T(8,128)(2,1)S(1)} %convert_bitcast_fusion) | data formatting | bytes 12582912 | tf_op jit(solution)/shard_map/reshape | solution.py:35
  131.4 0.0 copy-start.2
  131.4 0.0 copy-start.3
  131.4 3.8 %all-to-all-start.1 = ((bf16[1,8,192,2048]{3,1,0,2:T(8,128)(2,1)}), bf16[1,8,192,2048]{3,1,0,2:T(8,128)(2,1)}, u32[]{:S(2)}, u32[]{:S(2)}) async-start(bf16[1,8,192,2048]{3,1,0,2:T(8,128)(2,1)} %copy.42), calls=%async_computation.1 | async-start | bytes 12582912 | tf_op jit(solution)/shard_map/all_to_all | solution.py:36
  135.2 0.0 copy-done.2
  135.2 0.1 copy.44
  135.3 0.1 mul.64
  135.4 0.1 copy.40
  135.6 0.0 copy-done.3
  135.6 0.1 copy.35
  135.7 70.8 %all-to-all-done.1 = bf16[1,8,192,2048]{3,1,0,2:T(8,128)(2,1)} async-done(((bf16[1,8,192,2048]{3,1,0,2:T(8,128)(2,1)}), bf16[1,8,192,2048]{3,1,0,2:T(8,128)(2,1)}, u32[]{:S(2)}, u32[]{:S(2)}) %all-to-all-start.1) | async-done | bytes 6291488 | tf_op jit(solution)/shard_map/all_to_all | solution.py:36
  206.5 9.5 %copy.43 = bf16[1,8,8,24,2048]{4,3,1,2,0:T(8,128)(2,1)} copy(bf16[1,8,8,24,2048]{4,1,3,2,0:T(8,128)(2,1)} %bitcast.6) | data formatting | bytes 12582912 | tf_op jit(solution)/shard_map/all_to_all | solution.py:36
  216.0 8.0 %gather_fusion = bf16[288,2048]{1,0:T(8,128)(2,1)S(1)} fusion(bf16[1536,2048]{1,0:T(8,128)(2,1)} %bitcast.39, s32[1024]{0:T(1024)S(1)} %pad_clamp_fusion), kind=kCustom, calls=%fused_computation | custom fusion | bytes 2360448 | tf_op jit(solution)/shard_map/jit(_take)/gather | solution.py:38
  224.0 0.4 gather.7
  224.5 2.8 %multiply_reduce_fusion = bf16[48,2048]{1,0:T(8,128)(2,1)} fusion(bf16[48,6,2048]{2,1,0:T(8,128)(2,1)S(1)} %gather.7, f32[48,6]{1,0:T(8,128)S(1)} %copy.35, pred[48,6]{1,0:T(8,128)(4,1)S(1)} %copy.40), kind=kLoop, calls=%fused_computation.16 | loop fusion | flops 2260992 | bytes 1377696 | tf_op jit(solution)/shard_map/reduce_sum | solution.py:39
  227.3 0.0 copy-done.1
  (8 shorter events, 0.1 us)
Async XLA Ops:
  0.0 3.6 %copy-start = (bf16[48,2048]{1,0:T(8,128)(2,1)S(1)}, bf16[48,2048]{1,0:T(8,128)(2,1)}, u32[]{:S(2)}) copy-start(bf16[48,2048]{1,0:T(8,128)(2,1)} %param.5) | copy-start | bytes 589828
  131.4 3.8 %copy-start.2 = (s32[48,6]{0,1:T(8,128)S(1)}, s32[48,6]{0,1:T(8,128)}, u32[]{:S(2)}) copy-start(s32[48,6]{0,1:T(8,128)} %param.6) | copy-start | bytes 3460
  131.4 4.1 %copy-start.3 = (f32[48,6]{0,1:T(8,128)S(1)}, f32[48,6]{0,1:T(8,128)}, u32[]{:S(2)}) copy-start(f32[48,6]{0,1:T(8,128)} %param.7) | copy-start | bytes 3460
  131.4 75.1 %all-to-all-start.1 = ((bf16[1,8,192,2048]{3,1,0,2:T(8,128)(2,1)}), bf16[1,8,192,2048]{3,1,0,2:T(8,128)(2,1)}, u32[]{:S(2)}, u32[]{:S(2)}) async-start(bf16[1,8,192,2048]{3,1,0,2:T(8,128)(2,1)} %copy.42), calls=%async_computation.1 | async-start | bytes 12582912 | tf_op jit(solution)/shard_map/all_to_all | solution.py:36
  216.0 11.3 %copy-start.1 = (bf16[48,2048]{1,0:T(8,128)(2,1)S(1)}, bf16[48,2048]{1,0:T(8,128)(2,1)}, u32[]{:S(2)}) copy-start(bf16[48,2048]{1,0:T(8,128)(2,1)} %param.5) | copy-start | bytes 589828
where the time goes:
time: 228 us; the launch traced here: 227 us
  blocking collectives  75.6 us (33%)
  waiting for transfers between devices  70.8 us (31%)
  matrix products  42.9 us (19%)
  local copies, waits for them, and re-layouts  29.1 us (13%)
  other arithmetic  5.07 us (2%)
  starting transfers between devices  3.78 us (2%)
    all_to_all x1, blocking collectives, local_layer(): recv_rows = lax.all_to_all(send_rows, 'ep', 0, 2, tiled=True)  75.6 us
    all_to_all x1, waiting for transfers between devices, local_layer(): back_rows = lax.all_to_all(expert_out, 'ep', 2, 0, tiled=True)  70.8 us
    dot_general x1, matrix products, local_layer(): jnp.einsum('ecm,emf->ecf', recv_rows, w_up, preferred_element_type=jnp.fl...  22.3 us
    dot_general x1, matrix products, local_layer(): jnp.einsum('ecf,efm->ecm', hidden, w_down, preferred_element_type=jnp.flo...  18.7 us
    all_to_all x1, local copies, waits for them, and re-layouts, local_layer(): back_rows = lax.all_to_all(expert_out, 'ep', 2, 0, tiled=True)  9.51 us
    gather x2, local copies, waits for them, and re-layouts, local_layer(): jnp.take(back_rows, slot_ids, axis=0).reshape(tok_n, top_n, model_dim)  8.45 us
    reshape x1, local copies, waits for them, and re-layouts, local_layer(): expert_out.reshape(1, local_experts, group * slot_cap, model_dim)  6.1 us
  transfers between devices with their start and end apart: 1, of which 1 were waited for; matrix products, arithmetic and copies ran while one was open for 0% of the time, Pallas kernels for 0%

commit v1 on v0

v1 whole, which is shorter than its diff:
```python
import functools

import jax
import jax.numpy as jnp
from jax import lax
from jax.experimental import pallas as pl
from jax.experimental.pallas import tpu as pltpu
from jax.sharding import PartitionSpec as P

MESH = pl.DeviceIdType.MESH
F32 = jnp.float32
BF16 = jnp.bfloat16

UP_SLOTS = 3
DOWN_SLOTS = 4
COLS = 256


def gelu(z):
    inner = 0.7978845608028654 * (z + 0.044715 * (z * z * z))
    return 0.5 * z * (1.0 + jnp.tanh(inner))


def moe_kernel(dims, x_hbm, ids_hbm, gates_hbm, up_hbm, down_hbm, out_ref,
               up_buf, down_buf, ids_v, gates_v, x_all, meta_all, slots, hidden, mix, expert_out,
               part_own, part_send, part_recv, part_in,
               up_sem, down_sem, in_sem, disp_send, disp_recv, fwd_send, fwd_recv,
               pair_send, pair_recv, red_send, red_recv):
    tok, top_n, dim, ff, n_exp, cap = dims
    pair = 2 * tok
    per_exp = 2 * cap
    lanes_n = n_exp * per_exp
    n_blk = dim // COLS
    dp = lax.axis_index('dp')
    me = lax.axis_index('ep')
    core = lax.rem(me, 2)
    chip = me // 2
    cx = lax.rem(chip, 2)
    cy = chip // 2

    def dev(rel, other_core):
        xx = 1 - cx if rel % 2 else cx
        yy = 1 - cy if rel // 2 else cy
        cc = 1 - core if other_core else core
        return (dp, (yy * 2 + xx) * 2 + cc)

    partner = dev(0, True)

    copy_x = pltpu.make_async_copy(x_hbm, x_all.at[0, pl.ds(0, tok)], in_sem.at[0])
    copy_ids = pltpu.make_async_copy(ids_hbm, ids_v, in_sem.at[1])
    copy_gates = pltpu.make_async_copy(gates_hbm, gates_v, in_sem.at[2])
    copy_ids.start()
    copy_gates.start()
    copy_x.start()

    def up_copy(e, slot):
        return pltpu.make_async_copy(up_hbm.at[e], up_buf.at[slot], up_sem.at[slot])

    def down_copy(b, slot):
        return pltpu.make_async_copy(
            down_hbm.at[:, :, pl.ds(b * COLS, COLS)], down_buf.at[slot], down_sem.at[slot])

    for s in range(UP_SLOTS):
        up_copy(s, s).start()
    for s in range(DOWN_SLOTS):
        down_copy(s, s).start()

    barrier = pltpu.get_barrier_semaphore()
    pl.semaphore_signal(barrier, inc=1, device_id=partner, device_id_type=MESH)
    for rel in (1, 2, 3):
        pl.semaphore_signal(barrier, inc=1, device_id=dev(rel, False), device_id_type=MESH)

    copy_ids.wait()
    copy_gates.wait()
    lane = lax.broadcasted_iota(jnp.int32, (tok, 128), 1)
    chosen = jnp.zeros((tok, 128), F32)
    dense_gate = jnp.zeros((tok, 128), F32)
    for j in range(top_n):
        id_j = ids_v[:, j:j + 1]
        w_j = gates_v[:, j:j + 1]
        chosen = jnp.where(lane == id_j, 1.0, chosen)
        dense_gate = jnp.where(lane == id_j + 64, w_j, dense_gate)
    row_i = lax.broadcasted_iota(jnp.int32, (tok, tok), 0)
    col_i = lax.broadcasted_iota(jnp.int32, (tok, tok), 1)
    lower = jnp.where(col_i < row_i, 1.0, 0.0).astype(BF16)
    rank = jnp.dot(lower, chosen.astype(BF16), preferred_element_type=F32)
    meta_all[0, 0:tok, :] = jnp.where(lane < 64, jnp.where(chosen > 0.5, rank, -1.0), dense_gate)
    copy_x.wait()

    pl.semaphore_wait(barrier, 4)

    def dispatch(rel, what):
        ref = x_all if what == 0 else meta_all
        return pltpu.make_async_remote_copy(
            src_ref=ref.at[0, pl.ds(0, tok)], dst_ref=ref.at[rel, pl.ds(0, tok)],
            send_sem=disp_send.at[what, rel], recv_sem=disp_recv.at[what, rel],
            device_id=dev(rel, False), device_id_type=MESH)

    def forward(rel, what):
        ref = x_all if what == 0 else meta_all
        return pltpu.make_async_remote_copy(
            src_ref=ref.at[rel, pl.ds(0, tok)], dst_ref=ref.at[rel, pl.ds(tok, tok)],
            send_sem=fwd_send.at[what, rel], recv_sem=fwd_recv.at[what, rel],
            device_id=partner, device_id_type=MESH)

    for rel in (3, 1, 2):
        dispatch(rel, 1).start()
        dispatch(rel, 0).start()
    forward(0, 1).start()
    forward(0, 0).start()

    e_row = lax.broadcasted_iota(jnp.int32, (128, lanes_n), 0)
    e_col = lax.broadcasted_iota(jnp.int32, (128, lanes_n), 1)
    k_rank = (e_row - n_exp * me) * per_exp
    k_gate = k_rank - 64 * per_exp
    pick_rank = jnp.where((e_col >= k_rank) & (e_col < k_rank + per_exp), 1.0, 0.0).astype(BF16)
    pick_gate = jnp.where((e_col >= k_gate) & (e_col < k_gate + per_exp), 1.0, 0.0).astype(BF16)
    slot_f = lax.broadcasted_iota(jnp.int32, (pair, lanes_n), 1).astype(F32)
    tok_i = lax.broadcasted_iota(jnp.int32, (pair, lanes_n), 0)
    seg = jnp.floor((slot_f + 0.5) * (1.0 / cap))
    want = slot_f - cap * seg
    half = seg - 2.0 * jnp.floor((seg + 0.5) * 0.5)
    own_half = jnp.where(tok_i >= tok, 1.0, 0.0)
    want = jnp.where(half == own_half, want, -2.0)

    def place(rel):
        meta = meta_all[rel]
        g1 = meta.astype(BF16)
        left = meta - g1.astype(F32)
        g2 = left.astype(BF16)
        g3 = (left - g2.astype(F32)).astype(BF16)
        rank_e = jnp.dot(g1, pick_rank, preferred_element_type=F32)
        hit = rank_e == want
        for i, g in enumerate((g1, g2, g3)):
            g_e = jnp.dot(g, pick_gate, preferred_element_type=F32)
            mix[rel, i * pair:(i + 1) * pair, :] = jnp.where(hit, g_e, 0.0).astype(BF16)
        one_hot = jnp.where(hit, 1.0, 0.0).astype(BF16)
        step = 512
        for c in range(dim // step):
            rows = lax.dot_general(one_hot, x_all[rel, :, c * step:(c + 1) * step],
                                   (((0,), (0,)), ((), ())), preferred_element_type=F32).astype(BF16)
            for e in range(n_exp):
                slots[e, rel * per_exp:(rel + 1) * per_exp, c * step:(c + 1) * step] = (
                    rows[e * per_exp:(e + 1) * per_exp])

    forward(0, 1).wait_recv()
    forward(0, 0).wait_recv()
    place(0)
    for rel in (1, 2, 3):
        dispatch(rel, 1).wait_recv()
        forward(rel, 1).start()
        dispatch(rel, 0).wait_recv()
        forward(rel, 0).start()
    for rel in (1, 2, 3):
        forward(rel, 1).wait_recv()
        forward(rel, 0).wait_recv()
        place(rel)

    def up_step(e, carry):
        slot = lax.rem(e, UP_SLOTS)
        up_copy(e, slot).wait()
        base = 0
        while base < ff:
            width = min(512, ff - base)
            z = jnp.dot(slots[e], up_buf[slot, :, base:base + width], preferred_element_type=F32)
            hidden[e, :, base:base + width] = gelu(z).astype(BF16)
            base += width

        @pl.when(e + UP_SLOTS < n_exp)
        def _():
            up_copy(e + UP_SLOTS, slot).start()
        return carry

    lax.fori_loop(0, n_exp, up_step, 0)

    def pair_copy(b):
        return pltpu.make_async_remote_copy(
            src_ref=part_send.at[b], dst_ref=part_recv.at[b],
            send_sem=pair_send.at[b], recv_sem=pair_recv.at[b],
            device_id=partner, device_id_type=MESH)

    def reduce_copy(b, rel):
        return pltpu.make_async_remote_copy(
            src_ref=part_own.at[b, rel], dst_ref=part_in.at[b, rel - 1],
            send_sem=red_send.at[b, rel - 1], recv_sem=red_recv.at[b, rel - 1],
            device_id=dev(rel, False), device_id_type=MESH)

    def reduce_block(b):
        pair_copy(b).wait_recv()
        part_own[b] = part_own[b] + part_recv[b]
        for rel in (3, 1, 2):
            reduce_copy(b, rel).start()

    def down_step(b, carry):
        slot = lax.rem(b, DOWN_SLOTS)
        down_copy(b, slot).wait()
        for e in range(n_exp):
            o = jnp.dot(hidden[e], down_buf[slot, e], preferred_element_type=F32).astype(BF16)
            for rel in range(4):
                expert_out[rel, e * per_exp:(e + 1) * per_exp, :] = o[rel * per_exp:(rel + 1) * per_exp]

        @pl.when(b + DOWN_SLOTS < n_blk)
        def _():
            down_copy(b + DOWN_SLOTS, slot).start()

        for rel in range(4):
            y3 = jnp.dot(mix[rel], expert_out[rel], preferred_element_type=F32)
            y = y3[0:pair] + (y3[pair:2 * pair] + y3[2 * pair:3 * pair])
            part_own[b, rel] = y[0:tok]
            part_send[b, rel] = y[tok:pair]
        pair_copy(b).start()

        @pl.when(b > 0)
        def _():
            reduce_block(b - 1)
        return carry

    lax.fori_loop(0, n_blk, down_step, 0)
    reduce_block(n_blk - 1)

    def finish(b, carry):
        total = part_own[b, 0]
        for rel in (1, 2, 3):
            reduce_copy(b, rel).wait_recv()
            total = total + part_in[b, rel - 1]
        out_ref[:, pl.ds(pl.multiple_of(b * COLS, COLS), COLS)] = total.astype(BF16)
        return carry

    lax.fori_loop(0, n_blk, finish, 0)

    for what in (0, 1):
        for rel in (1, 2, 3):
            dispatch(rel, what).wait_send()
        for rel in range(4):
            forward(rel, what).wait_send()

    def drain(b, carry):
        pair_copy(b).wait_send()
        for rel in (1, 2, 3):
            reduce_copy(b, rel).wait_send()
        return carry

    lax.fori_loop(0, n_blk, drain, 0)


def solution(mesh):
    token_spec = P(('dp', 'ep'), None)
    expert_spec = P('ep', None, None)

    def local_layer(x_loc, ids_loc, gates_loc, w_up, w_down):
        tok, top_n = ids_loc.shape
        dim = x_loc.shape[1]
        n_exp, _, ff = w_up.shape
        cap = tok // 2
        pair = 2 * tok
        lanes_n = n_exp * 2 * cap
        n_blk = dim // COLS
        rows = 8 * cap
        dims = (tok, top_n, dim, ff, n_exp, cap)
        dma = pltpu.SemaphoreType.DMA
        hbm = pl.BlockSpec(memory_space=pl.ANY)
        return pl.pallas_call(
            functools.partial(moe_kernel, dims),
            out_shape=jax.ShapeDtypeStruct((tok, dim), BF16),
            in_specs=[hbm] * 5,
            out_specs=pl.BlockSpec(memory_space=pltpu.VMEM),
            scratch_shapes=[
                pltpu.VMEM((UP_SLOTS, dim, ff), BF16),
                pltpu.VMEM((DOWN_SLOTS, n_exp, ff, COLS), BF16),
                pltpu.VMEM((tok, top_n), jnp.int32),
                pltpu.VMEM((tok, top_n), F32),
                pltpu.VMEM((4, pair, dim), BF16),
                pltpu.VMEM((4, pair, 128), F32),
                pltpu.VMEM((n_exp, rows, dim), BF16),
                pltpu.VMEM((n_exp, rows, ff), BF16),
                pltpu.VMEM((4, 3 * pair, lanes_n), BF16),
                pltpu.VMEM((4, lanes_n, COLS), BF16),
                pltpu.VMEM((n_blk, 4, tok, COLS), F32),
                pltpu.VMEM((n_blk, 4, tok, COLS), F32),
                pltpu.VMEM((n_blk, 4, tok, COLS), F32),
                pltpu.VMEM((n_blk, 3, tok, COLS), F32),
                dma((UP_SLOTS,)), dma((DOWN_SLOTS,)), dma((3,)),
                dma((2, 4)), dma((2, 4)), dma((2, 4)), dma((2, 4)),
                dma((n_blk,)), dma((n_blk,)), dma((n_blk, 3)), dma((n_blk, 3)),
            ],
            compiler_params=pltpu.CompilerParams(
                collective_id=0, has_side_effects=True, vmem_limit_bytes=67043328),
            name='moe_layer',
        )(x_loc, ids_loc, gates_loc, w_up, w_down)

    return jax.shard_map(local_layer, mesh=mesh, in_specs=(token_spec, token_spec, token_spec, expert_spec, expert_spec),
                         out_specs=token_spec, check_vma=False)
```

time: 228 us -> 68.6 us (0.30)
  blocking collectives: 75.6 us -> 0 us
  waiting for transfers between devices: 70.8 us -> 0 us
  Pallas kernels: 0 us -> 64 us
  matrix products: 42.9 us -> 0 us
  local copies, waits for them, and re-layouts: 29.1 us -> 4.36 us
  other arithmetic: 5.07 us -> 0 us
  starting transfers between devices: 3.78 us -> 0 us
    all_to_all x1 -> x0, blocking collectives: 75.6 us -> none  [local_layer(): recv_rows = lax.all_to_all(send_rows, 'ep', 0, 2, tiled=True)]
    all_to_all x1 -> x0, waiting for transfers between devices: 70.8 us -> none  [local_layer(): back_rows = lax.all_to_all(expert_out, 'ep', 2, 0, tiled=True)]
    pallas_call x0 -> x1, Pallas kernels: none -> 64 us  [local_layer(): pl.pallas_call(functools.partial(moe_kernel, dims), out_shape=jax.ShapeDt...]
    dot_general x3 -> x0, matrix products: 42.9 us -> none  [the longest x1 22.3 us: local_layer(): jnp.einsum('ecm,emf->ecf', recv_rows, w_up, preferred_element_type=jnp.fl...]
    all_to_all x2 -> x0, local copies, waits for them, and re-layouts: 12.7 us -> none  [the longest x1 9.51 us: local_layer(): back_rows = lax.all_to_all(expert_out, 'ep', 2, 0, tiled=True)]
    gather x2 -> x0, local copies, waits for them, and re-layouts: 8.45 us -> none  [local_layer(): jnp.take(back_rows, slot_ids, axis=0).reshape(tok_n, top_n, model_dim)]
    reshape x2 -> x0, local copies, waits for them, and re-layouts: 6.22 us -> none  [the longest x1 6.1 us: local_layer(): expert_out.reshape(1, local_experts, group * slot_cap, model_dim)]
    all_to_all x1 -> x0, starting transfers between devices: 3.78 us -> none  [local_layer(): back_rows = lax.all_to_all(expert_out, 'ep', 2, 0, tiled=True)]
  transfers between devices with their start and end apart: 1 -> 0, of which waited for: 1 -> 0; matrix products, arithmetic and copies ran while one was open for 0% -> 0% of each run, Pallas kernels for 0% -> 0%
where the time goes in v1:
time: 68.6 us; the launch traced here: 68.4 us
  Pallas kernels  64 us (93%)
  local copies, waits for them, and re-layouts  4.36 us (6%)
    pallas_call x1, Pallas kernels, local_layer(): pl.pallas_call(functools.partial(moe_kernel, dims), out_shape=jax.ShapeDt...  64 us
    unnamed x3, local copies, waits for them, and re-layouts  4.36 us

profile of v1, /device:TPU:0, one launch (start us, length us, event | category | flops | bytes accessed | tf_op | source)
XLA Modules:
  0.0 68.4 jit_solution(17628193092461605219)
XLA Ops:
  0.0 1.4 %copy.6.ids_hbm = s32[48,6]{1,0:T(8,128)} copy(s32[48,6]{0,1:T(8,128)} %param.6) | data formatting | bytes 2304 | tf_op args[1]
  1.4 1.4 %copy.7.gates_hbm = f32[48,6]{1,0:T(8,128)} copy(f32[48,6]{0,1:T(8,128)} %param.7) | data formatting | bytes 2304 | tf_op args[2]
  2.7 64.0 %moe_layer.1 = bf16[48,2048]{1,0:T(8,128)(2,1)} custom-call(bf16[48,2048]{1,0:T(8,128)(2,1)} %x_hbm.1, s32[48,6]{1,0:T(8,128)} %copy.6.ids_hbm, f32[48,6]{1,0:T(8,128)} %copy.7.gates_hbm, bf16[8,2048,1408]{2,1,0:T(8,128)(2,1)} %up_hbm.1, bf16[8,1408,2048]{2,1,0:T(8,128)(2,1)} %down_hbm.1), custom_call_target="tpu_custom_call" | custom-call | tf_op jit(solution)/shard_map/moe_layer/pallas_call | solution.py:262
  66.8 1.6 %copy.9 = bf16[48,2048]{1,0:T(8,128)(2,1)} copy(bf16[48,2048]{1,0:T(8,128)(2,1)} %moe_layer.1) | data formatting | bytes 393216

commit v2 on v0

v2 whole, which is shorter than its diff:
```python
import functools

import jax
import jax.numpy as jnp
from jax import lax
from jax.experimental import pallas as pl
from jax.experimental.pallas import tpu as pltpu
from jax.sharding import PartitionSpec as P

MESH = pl.DeviceIdType.MESH
F32 = jnp.float32
BF16 = jnp.bfloat16

UP_SLOTS = 6
EARLY = 4
RING = UP_SLOTS // 2
PER_SLOT = 5
COLS = 256
HALF = COLS // 2
CHUNKS = 4


def gelu(z):
    inner = 0.7978845608028654 * (z + 0.044715 * (z * z * z))
    return 0.5 * z * (1.0 + jnp.tanh(inner))


def moe_kernel(dims, x_hbm, ids_hbm, gates_hbm, up_hbm, down_hbm, out_hbm,
               up_buf, first_buf, out_v, ids_v, gates_v, x_all, meta_all, one_hot, slots, acc, hidden, mix, expert_out,
               part_own, part_send, part_recv, in_x1, in_y1, in_x2, in_y2, in_last,
               up_sem, first_sem, down_sem, out_sem, in_sem, meta_send, meta_recv, tok_send, tok_recv, diag_send, diag_recv,
               mpair_send, mpair_recv, tpair_send, tpair_recv,
               pair_send, pair_recv, red_send, red_recv, last_send, last_recv):
    tok, top_n, dim, ff, n_exp, cap = dims
    pair = 2 * tok
    per_exp = 2 * cap
    lanes_n = n_exp * per_exp
    n_blk = dim // COLS
    chunk = dim // CHUNKS
    dp = lax.axis_index('dp')
    me = lax.axis_index('ep')
    core = lax.rem(me, 2)
    chip = me // 2
    cx = lax.rem(chip, 2)
    cy = chip // 2

    def dev(rel, other_core):
        xx = 1 - cx if rel % 2 else cx
        yy = 1 - cy if rel // 2 else cy
        cc = 1 - core if other_core else core
        return (dp, (yy * 2 + xx) * 2 + cc)

    partner = dev(0, True)

    barrier = pltpu.get_barrier_semaphore()
    for rel in (3, 1, 2):
        pl.semaphore_signal(barrier, inc=1, device_id=dev(rel, False), device_id_type=MESH)
    pl.semaphore_signal(barrier, inc=1, device_id=partner, device_id_type=MESH)

    copy_x = pltpu.make_async_copy(x_hbm, x_all.at[0, pl.ds(0, tok)], in_sem.at[0])
    copy_ids = pltpu.make_async_copy(ids_hbm, ids_v, in_sem.at[1])
    copy_gates = pltpu.make_async_copy(gates_hbm, gates_v, in_sem.at[2])
    copy_x.start()
    copy_ids.start()
    copy_gates.start()

    def up_copy(e):
        slot = lax.rem(e, UP_SLOTS)
        return pltpu.make_async_copy(up_hbm.at[e], up_buf.at[slot], up_sem.at[slot])

    first_copy = pltpu.make_async_copy(down_hbm.at[:, :, pl.ds(0, COLS)], first_buf, first_sem.at[0])

    def down_place(b, e):
        return 2 * lax.rem(b, RING) + e // PER_SLOT, (e % PER_SLOT) * COLS

    def down_copy(b, e):
        slot, col = down_place(b, e)
        return pltpu.make_async_copy(
            down_hbm.at[e, :, pl.ds(pl.multiple_of(b * COLS, COLS), COLS)], up_buf.at[slot, pl.ds(0, ff), pl.ds(col, COLS)],
            down_sem.at[lax.rem(b, RING), e])

    def down_start(b):
        for e in range(n_exp):
            down_copy(b, e).start()

    copy_ids.wait()
    copy_gates.wait()
    copy_x.wait()
    for e in range(UP_SLOTS):
        up_copy(e).start()
    first_copy.start()

    def remote(src, dst, send, recv, to):
        return pltpu.make_async_remote_copy(
            src_ref=src, dst_ref=dst, send_sem=send, recv_sem=recv, device_id=to, device_id_type=MESH)

    def meta_out(rel):
        return remote(meta_all.at[0, pl.ds(0, tok)], meta_all.at[rel, pl.ds(0, tok)],
                      meta_send.at[rel], meta_recv.at[rel], dev(rel, False))

    def meta_pair(rel):
        return remote(meta_all.at[rel, pl.ds(0, tok)], meta_all.at[rel, pl.ds(tok, tok)],
                      mpair_send.at[rel], mpair_recv.at[rel], partner)

    def tok_out(rel, c):
        cols = pl.ds(c * chunk, chunk)
        return remote(x_all.at[0, pl.ds(0, tok), cols], x_all.at[rel, pl.ds(0, tok), cols],
                      tok_send.at[rel, c], tok_recv.at[rel, c], dev(rel, False))

    def tok_diag(via, c):
        cols = pl.ds(c * chunk + (via - 1) * (chunk // 2), chunk // 2)
        return remote(x_all.at[via, pl.ds(0, tok), cols], x_all.at[3, pl.ds(0, tok), cols],
                      diag_send.at[via, c], diag_recv.at[via, c], dev(3 - via, False))

    def tok_pair(rel, c):
        cols = pl.ds(c * chunk, chunk)
        return remote(x_all.at[rel, pl.ds(0, tok), cols], x_all.at[rel, pl.ds(tok, tok), cols],
                      tpair_send.at[rel, c], tpair_recv.at[rel, c], partner)

    pl.semaphore_wait(barrier, 4)
    tok_out(1, 0).start()
    tok_out(2, 0).start()
    for c in range(CHUNKS):
        tok_pair(0, c).start()

    sub = lax.broadcasted_iota(jnp.int32, (64, tok), 0)
    chosen = jnp.zeros((64, tok), F32)
    dense_gate = jnp.zeros((64, tok), F32)
    for j in range(top_n):
        same = sub == ids_v[j:j + 1, :]
        chosen = jnp.where(same, 1.0, chosen)
        dense_gate = jnp.where(same, gates_v[j:j + 1, :], dense_gate)
    row_i = lax.broadcasted_iota(jnp.int32, (tok, tok), 0)
    col_i = lax.broadcasted_iota(jnp.int32, (tok, tok), 1)
    before = jnp.where(row_i < col_i, 1.0, 0.0).astype(BF16)
    rank = jnp.dot(chosen.astype(BF16), before, preferred_element_type=F32)
    meta_t = jnp.concatenate([jnp.where(chosen > 0.5, rank, -1.0), dense_gate], axis=0)
    meta_all[0, 0:tok, :] = meta_t.T
    for rel in (3, 1, 2):
        meta_out(rel).start()
    meta_pair(0).start()
    for c in (1, 2):
        tok_out(1, c).start()
        tok_out(2, c).start()

    e_row = lax.broadcasted_iota(jnp.int32, (128, lanes_n), 0)
    e_col = lax.broadcasted_iota(jnp.int32, (128, lanes_n), 1)
    k_rank = (e_row - n_exp * me) * per_exp
    k_gate = k_rank - 64 * per_exp
    pick_rank = jnp.where((e_col >= k_rank) & (e_col < k_rank + per_exp), 1.0, 0.0).astype(BF16)
    pick_gate = jnp.where((e_col >= k_gate) & (e_col < k_gate + per_exp), 1.0, 0.0).astype(BF16)
    slot_f = lax.broadcasted_iota(jnp.int32, (pair, lanes_n), 1).astype(F32)
    tok_i = lax.broadcasted_iota(jnp.int32, (pair, lanes_n), 0)
    seg = jnp.floor((slot_f + 0.5) * (1.0 / cap))
    want = slot_f - cap * seg
    half = seg - 2.0 * jnp.floor((seg + 0.5) * 0.5)
    own_half = jnp.where(tok_i >= tok, 1.0, 0.0)
    want = jnp.where(half == own_half, want, -2.0)

    def masks(rels):
        for rel in rels:
            meta_pair(rel).wait_recv()
        for rel in rels:
            meta = meta_all[rel]
            g1 = meta.astype(BF16)
            left = meta - g1.astype(F32)
            g2 = left.astype(BF16)
            g3 = (left - g2.astype(F32)).astype(BF16)
            rank_e = jnp.dot(g1, pick_rank, preferred_element_type=F32)
            hit = rank_e == want
            for i, g in enumerate((g1, g2, g3)):
                g_e = jnp.dot(g, pick_gate, preferred_element_type=F32)
                mix[rel, i * pair:(i + 1) * pair, :] = jnp.where(hit, g_e, 0.0).astype(BF16)
            one_hot[rel] = jnp.where(hit, 1.0, 0.0).astype(BF16)

    def arrived(c):
        for via in (1, 2):
            tok_out(via, c).wait_recv()
            tok_diag(via, c).start()
            tok_pair(via, c).start()

    def diag_arrived(c):
        for via in (1, 2):
            tok_diag(via, c).wait_recv()
        tok_pair(3, c).start()

    def place(rels, cs):
        for c in cs:
            for rel in rels:
                tok_pair(rel, c).wait_recv()
        for c in cs:
            for rel in rels:
                rows = lax.dot_general(one_hot[rel], x_all[rel, :, c * chunk:(c + 1) * chunk],
                                       (((0,), (0,)), ((), ())), preferred_element_type=F32).astype(BF16)
                for e in range(n_exp):
                    slots[e, rel * per_exp:(rel + 1) * per_exp, c * chunk:(c + 1) * chunk] = (
                        rows[e * per_exp:(e + 1) * per_exp])

    def early(e):
        up_copy(e).wait()
        z = jnp.dot(slots[e, 0:per_exp, :], up_buf[e], preferred_element_type=F32)
        hidden[e, 0:per_exp, :] = gelu(z).astype(BF16)

    def late_dot(e, lo, hi):
        return jnp.dot(slots[e, per_exp:, lo:hi], up_buf[e, lo:hi, :], preferred_element_type=F32)

    def work_first():
        for e in range(EARLY):
            acc[e] = late_dot(e, 0, chunk)

    def work_second():
        for e in range(EARLY):
            acc[e] = acc[e] + late_dot(e, chunk, 2 * chunk)

    def work_third(e0, e1):
        for e in range(e0, e1):
            hidden[e, per_exp:, :] = gelu(acc[e] + late_dot(e, 2 * chunk, dim)).astype(BF16)
        for e in range(e0, e1):
            if e + UP_SLOTS < n_exp:
                up_copy(e + UP_SLOTS).start()

    def work_whole(e0, e1):
        for e in range(e0, e1):
            up_copy(e).wait()
        for e in range(e0, e1):
            z = jnp.dot(slots[e], up_buf[e % UP_SLOTS], preferred_element_type=F32)
            hidden[e] = gelu(z).astype(BF16)

    masks((0,))
    place((0,), range(CHUNKS))
    early(0)
    early(1)
    arrived(0)
    tok_out(1, 3).start()
    tok_out(2, 3).start()
    early(2)
    for rel in (1, 2, 3):
        meta_out(rel).wait_recv()
        meta_pair(rel).start()
    arrived(1)
    early(3)
    arrived(2)
    masks((1, 2, 3))
    diag_arrived(0)
    place((1, 2), (0,))
    arrived(3)
    diag_arrived(1)
    place((3,), (0,))
    work_first()
    diag_arrived(2)
    diag_arrived(3)
    place((1, 2, 3), (1,))
    work_second()
    place((1, 2, 3), (2, 3))
    work_third(0, 2)
    work_third(2, 4)
    down_start(1)
    work_whole(4, 6)
    down_start(2)
    work_whole(6, 8)
    down_start(3)

    def pair_copy(b):
        return remote(part_send.at[b], part_recv.at[b], pair_send.at[b], pair_recv.at[b], partner)

    lo, hi = pl.ds(0, HALF), pl.ds(HALF, HALF)
    everyone = pl.ds(0, 2)

    def first_x(b):
        return remote(part_own.at[b, everyone, 1, :, lo], in_x1.at[b], red_send.at[b, 0], red_recv.at[b, 0], dev(1, False))

    def first_y(b):
        return remote(part_own.at[b, 1, everyone, :, hi], in_y1.at[b], red_send.at[b, 1], red_recv.at[b, 1], dev(2, False))

    def second_y(b):
        return remote(part_own.at[b, 1, 0, :, lo], in_y2.at[b], red_send.at[b, 2], red_recv.at[b, 2], dev(2, False))

    def second_x(b):
        return remote(part_own.at[b, 0, 1, :, hi], in_x2.at[b], red_send.at[b, 3], red_recv.at[b, 3], dev(1, False))

    def stage_one(b):
        pair_copy(b).wait_recv()
        part_own[b] = part_own[b] + part_recv[b]
        first_x(b).start()
        first_y(b).start()

    def stage_two(b):
        first_x(b).wait_recv()
        part_own[b, 1, 0, :, 0:HALF] = part_own[b, 1, 0, :, 0:HALF] + in_x1[b, 1]
        second_y(b).start()
        first_y(b).wait_recv()
        part_own[b, 0, 1, :, HALF:COLS] = part_own[b, 0, 1, :, HALF:COLS] + in_y1[b, 1]
        second_x(b).start()

    def down_dot(e, weights):
        o = jnp.dot(hidden[e], weights, preferred_element_type=F32).astype(BF16)
        for rel in range(4):
            expert_out[rel, e * per_exp:(e + 1) * per_exp, :] = o[rel * per_exp:(rel + 1) * per_exp]

    def combine(b):
        for rel in range(4):
            y3 = jnp.dot(mix[rel], expert_out[rel], preferred_element_type=F32)
            y = y3[0:pair] + (y3[pair:2 * pair] + y3[2 * pair:3 * pair])
            part_own[b, rel // 2, rel % 2] = y[0:tok]
            part_send[b, rel // 2, rel % 2] = y[tok:pair]
        pair_copy(b).start()

    def down_first():
        first_copy.wait()
        for e in range(n_exp):
            down_dot(e, first_buf[e])
        combine(0)

    def down_step(b, carry):
        for e in range(n_exp):
            down_copy(b, e).wait()
        for e in range(n_exp):
            slot, col = down_place(b, e)
            down_dot(e, up_buf[slot, 0:ff, col:col + COLS])

        @pl.when(b + RING < n_blk)
        def _():
            down_start(b + RING)

        stage_one(b - 1)

        @pl.when(b > 2)
        def _():
            stage_two(b - 3)

        combine(b)
        return carry

    def out_copy(b):
        cols = pl.ds(pl.multiple_of(b * COLS, COLS), COLS)
        return pltpu.make_async_copy(out_v.at[b], out_hbm.at[:, cols], out_sem.at[b])

    def finish(b, carry):
        second_y(b).wait_recv()
        left = part_own[b, 0, 0, :, 0:HALF] + in_x1[b, 0] + in_y2[b]
        out_v[b, :, 0:HALF] = left.astype(BF16)
        second_x(b).wait_recv()
        right = part_own[b, 0, 0, :, HALF:COLS] + in_y1[b, 0] + in_x2[b]
        out_v[b, :, HALF:COLS] = right.astype(BF16)
        out_copy(b).start()
        return carry

    last = n_blk - 1

    def last_copy(rel):
        return remote(part_own.at[last, rel // 2, rel % 2], in_last.at[rel - 1],
                      last_send.at[rel - 1], last_recv.at[rel - 1], dev(rel, False))

    down_first()
    lax.fori_loop(1, n_blk, down_step, 0)
    stage_two(last - 2)
    lax.fori_loop(0, last - 4, finish, 0)
    pair_copy(last).wait_recv()
    part_own[last] = part_own[last] + part_recv[last]
    for rel in (3, 1, 2):
        last_copy(rel).start()
    stage_two(last - 1)
    lax.fori_loop(last - 4, last, finish, 0)
    for rel in (1, 2, 3):
        last_copy(rel).wait_recv()
    total = part_own[last, 0, 0] + in_last[0] + in_last[1] + in_last[2]
    out_v[last] = total.astype(BF16)
    out_copy(last).start()

    for rel in range(4):
        meta_pair(rel).wait_send()
        if rel:
            meta_out(rel).wait_send()
        for c in range(CHUNKS):
            tok_pair(rel, c).wait_send()
            if rel in (1, 2):
                tok_out(rel, c).wait_send()
                tok_diag(rel, c).wait_send()

    for rel in (1, 2, 3):
        last_copy(rel).wait_send()
    pair_copy(last).wait_send()

    def drain(b, carry):
        for copy in (pair_copy, first_x, first_y, second_x, second_y):
            copy(b).wait_send()
        return carry

    lax.fori_loop(0, last, drain, 0)
    def flush(b, carry):
        out_copy(b).wait()
        return carry

    lax.fori_loop(0, n_blk, flush, 0)


def solution(mesh):
    token_spec = P(('dp', 'ep'), None)
    expert_spec = P('ep', None, None)

    def local_layer(x_loc, ids_loc, gates_loc, w_up, w_down):
        tok, top_n = ids_loc.shape
        dim = x_loc.shape[1]
        n_exp, _, ff = w_up.shape
        cap = tok // 2
        pair = 2 * tok
        lanes_n = n_exp * 2 * cap
        n_blk = dim // COLS
        rows = 8 * cap
        dims = (tok, top_n, dim, ff, n_exp, cap)
        dma = pltpu.SemaphoreType.DMA
        hbm = pl.BlockSpec(memory_space=pl.ANY)
        return pl.pallas_call(
            functools.partial(moe_kernel, dims),
            out_shape=jax.ShapeDtypeStruct((tok, dim), BF16),
            in_specs=[hbm] * 5,
            out_specs=hbm,
            scratch_shapes=[
                pltpu.VMEM((UP_SLOTS, dim, ff), BF16),
                pltpu.VMEM((n_exp, ff, COLS), BF16),
                pltpu.VMEM((n_blk, tok, COLS), BF16),
                pltpu.VMEM((top_n, tok), jnp.int32),
                pltpu.VMEM((top_n, tok), F32),
                pltpu.VMEM((4, pair, dim), BF16),
                pltpu.VMEM((4, pair, 128), F32),
                pltpu.VMEM((4, pair, lanes_n), BF16),
                pltpu.VMEM((n_exp, rows, dim), BF16),
                pltpu.VMEM((EARLY, rows - 2 * cap, ff), F32),
                pltpu.VMEM((n_exp, rows, ff), BF16),
                pltpu.VMEM((4, 3 * pair, lanes_n), BF16),
                pltpu.VMEM((4, lanes_n, COLS), BF16),
                pltpu.VMEM((n_blk, 2, 2, tok, COLS), F32),
                pltpu.VMEM((n_blk, 2, 2, tok, COLS), F32),
                pltpu.VMEM((n_blk, 2, 2, tok, COLS), F32),
                pltpu.VMEM((n_blk, 2, tok, HALF), F32),
                pltpu.VMEM((n_blk, 2, tok, HALF), F32),
                pltpu.VMEM((n_blk, tok, HALF), F32),
                pltpu.VMEM((n_blk, tok, HALF), F32),
                pltpu.VMEM((3, tok, COLS), F32),
                dma((UP_SLOTS,)), dma((1,)), dma((RING, n_exp)), dma((n_blk,)), dma((3,)),
                dma((4,)), dma((4,)),
                dma((3, CHUNKS)), dma((3, CHUNKS)), dma((3, CHUNKS)), dma((3, CHUNKS)),
                dma((4,)), dma((4,)), dma((4, CHUNKS)), dma((4, CHUNKS)),
                dma((n_blk,)), dma((n_blk,)), dma((n_blk, 4)), dma((n_blk, 4)),
                dma((3,)), dma((3,)),
            ],
            compiler_params=pltpu.CompilerParams(
                collective_id=0, has_side_effects=True, vmem_limit_bytes=67043328),
            name='moe_layer',
        )(x_loc, ids_loc.T, gates_loc.T, w_up, w_down)

    return jax.shard_map(local_layer, mesh=mesh, in_specs=(token_spec, token_spec, token_spec, expert_spec, expert_spec),
                         out_specs=token_spec, check_vma=False)
```

time: 228 us -> 52.1 us (0.23)
  blocking collectives: 75.6 us -> 0 us
  waiting for transfers between devices: 70.8 us -> 0 us
  Pallas kernels: 0 us -> 50.3 us
  matrix products: 42.9 us -> 0 us
  local copies, waits for them, and re-layouts: 29.1 us -> 1.62 us
  other arithmetic: 5.07 us -> 0 us
  starting transfers between devices: 3.78 us -> 0 us
    all_to_all x1 -> x0, blocking collectives: 75.6 us -> none  [local_layer(): recv_rows = lax.all_to_all(send_rows, 'ep', 0, 2, tiled=True)]
    all_to_all x1 -> x0, waiting for transfers between devices: 70.8 us -> none  [local_layer(): back_rows = lax.all_to_all(expert_out, 'ep', 2, 0, tiled=True)]
    pallas_call x0 -> x1, Pallas kernels: none -> 50.3 us  [local_layer(): pl.pallas_call(functools.partial(moe_kernel, dims), out_shape=jax.ShapeDt...]
    dot_general x3 -> x0, matrix products: 42.9 us -> none  [the longest x1 22.3 us: local_layer(): jnp.einsum('ecm,emf->ecf', recv_rows, w_up, preferred_element_type=jnp.fl...]
    all_to_all x2 -> x0, local copies, waits for them, and re-layouts: 12.7 us -> none  [the longest x1 9.51 us: local_layer(): back_rows = lax.all_to_all(expert_out, 'ep', 2, 0, tiled=True)]
    gather x2 -> x0, local copies, waits for them, and re-layouts: 8.45 us -> none  [local_layer(): jnp.take(back_rows, slot_ids, axis=0).reshape(tok_n, top_n, model_dim)]
    reshape x2 -> x0, local copies, waits for them, and re-layouts: 6.22 us -> none  [the longest x1 6.1 us: local_layer(): expert_out.reshape(1, local_experts, group * slot_cap, model_dim)]
    all_to_all x1 -> x0, starting transfers between devices: 3.78 us -> none  [local_layer(): back_rows = lax.all_to_all(expert_out, 'ep', 2, 0, tiled=True)]
  transfers between devices with their start and end apart: 1 -> 0, of which waited for: 1 -> 0; matrix products, arithmetic and copies ran while one was open for 0% -> 0% of each run, Pallas kernels for 0% -> 0%
where the time goes in v2:
time: 52.1 us; the launch traced here: 52 us
  Pallas kernels  50.3 us (97%)
  local copies, waits for them, and re-layouts  1.62 us (3%)
    pallas_call x1, Pallas kernels, local_layer(): pl.pallas_call(functools.partial(moe_kernel, dims), out_shape=jax.ShapeDt...  50.3 us
    unnamed x1, local copies, waits for them, and re-layouts  1.62 us

profile of v2, /device:TPU:0, one launch (start us, length us, event | category | flops | bytes accessed | tf_op | source)
XLA Modules:
  0.0 52.0 jit_solution(4310049385961154003)
XLA Ops:
  0.0 50.3 %moe_layer.1 = bf16[48,2048]{1,0:T(8,128)(2,1)} custom-call(bf16[48,2048]{1,0:T(8,128)(2,1)} %x_hbm.1, s32[6,48]{1,0:T(8,128)} %bitcast.2, f32[6,48]{1,0:T(8,128)} %bitcast.3, bf16[8,2048,1408]{2,1,0:T(8,128)(2,1)} %up_hbm.1, bf16[8,1408,2048]{2,1,0:T(8,128)(2,1)} %down_hbm.1), custom_call_target="tpu_custom_call" | custom-call | tf_op jit(solution)/shard_map/moe_layer/pallas_call | solution.py:413
  50.3 1.6 %copy.7 = bf16[48,2048]{1,0:T(8,128)(2,1)} copy(bf16[48,2048]{1,0:T(8,128)(2,1)} %moe_layer.1) | data formatting | bytes 393216

commit v3 on v2

--- a/solution.py
+++ b/solution.py
@@ -25,12 +25,11 @@
     return 0.5 * z * (1.0 + jnp.tanh(inner))
 
 
-def moe_kernel(dims, x_hbm, ids_hbm, gates_hbm, up_hbm, down_hbm, out_hbm,
-               up_buf, first_buf, out_v, ids_v, gates_v, x_all, meta_all, one_hot, slots, acc, hidden, mix, expert_out,
-               part_own, part_send, part_recv, in_x1, in_y1, in_x2, in_y2, in_last,
-               up_sem, first_sem, down_sem, out_sem, in_sem, meta_send, meta_recv, tok_send, tok_recv, diag_send, diag_recv,
-               mpair_send, mpair_recv, tpair_send, tpair_recv,
-               pair_send, pair_recv, red_send, red_recv, last_send, last_recv):
+def moe_kernel(dims, x_hbm, ids_hbm, gates_hbm, up_hbm, down_hbm, out_ref,
+               up_buf, first_buf, ids_v, gates_v, x_all, meta_all, one_hot, slots, acc, hidden, mix, expert_out,
+               part_own, part_send, part_recv, in_x1, in_y1, in_two, in_last,
+               up_sem, first_sem, down_sem, in_sem, send_sem, meta_recv, mpair_recv,
+               tok_recv, diag_recv, tpair_recv, pair_recv, one_recv, two_recv, last_recv):
     tok, top_n, dim, ff, n_exp, cap = dims
     pair = 2 * tok
     per_exp = 2 * cap
@@ -77,11 +76,14 @@
         slot, col = down_place(b, e)
         return pltpu.make_async_copy(
             down_hbm.at[e, :, pl.ds(pl.multiple_of(b * COLS, COLS), COLS)], up_buf.at[slot, pl.ds(0, ff), pl.ds(col, COLS)],
-            down_sem.at[lax.rem(b, RING), e])
+            down_sem.at[lax.rem(b, RING)])
 
     def down_start(b):
         for e in range(n_exp):
             down_copy(b, e).start()
+
+    def down_wait(b):
+        pltpu.make_async_copy(down_hbm.at[:, :, pl.ds(0, COLS)], first_buf, down_sem.at[lax.rem(b, RING)]).wait()
 
     copy_ids.wait()
     copy_gates.wait()
@@ -94,34 +96,43 @@
         return pltpu.make_async_remote_copy(
             src_ref=src, dst_ref=dst, send_sem=send, recv_sem=recv, device_id=to, device_id_type=MESH)
 
+    meta_sent, tok_sent, pair_sent, one_sent, two_sent, last_sent = (send_sem.at[i] for i in range(6))
+
     def meta_out(rel):
         return remote(meta_all.at[0, pl.ds(0, tok)], meta_all.at[rel, pl.ds(0, tok)],
-                      meta_send.at[rel], meta_recv.at[rel], dev(rel, False))
+                      meta_sent, meta_recv.at[rel - 1], dev(rel, False))
 
     def meta_pair(rel):
         return remote(meta_all.at[rel, pl.ds(0, tok)], meta_all.at[rel, pl.ds(tok, tok)],
-                      mpair_send.at[rel], mpair_recv.at[rel], partner)
+                      meta_sent, mpair_recv.at[min(rel, 1)], partner)
 
     def tok_out(rel, c):
         cols = pl.ds(c * chunk, chunk)
         return remote(x_all.at[0, pl.ds(0, tok), cols], x_all.at[rel, pl.ds(0, tok), cols],
-                      tok_send.at[rel, c], tok_recv.at[rel, c], dev(rel, False))
+                      tok_sent, tok_recv.at[rel - 1, c], dev(rel, False))
 
     def tok_diag(via, c):
         cols = pl.ds(c * chunk + (via - 1) * (chunk // 2), chunk // 2)
         return remote(x_all.at[via, pl.ds(0, tok), cols], x_all.at[3, pl.ds(0, tok), cols],
-                      diag_send.at[via, c], diag_recv.at[via, c], dev(3 - via, False))
+                      tok_sent, diag_recv.at[c], dev(3 - via, False))
 
     def tok_pair(rel, c):
         cols = pl.ds(c * chunk, chunk)
         return remote(x_all.at[rel, pl.ds(0, tok), cols], x_all.at[rel, pl.ds(tok, tok), cols],
-                      tpair_send.at[rel, c], tpair_recv.at[rel, c], partner)
+                      tok_sent, tpair_recv.at[0 if rel == 3 else 1, c], partner)
+
+    own_pair = remote(x_all.at[0, pl.ds(0, tok)], x_all.at[0, pl.ds(tok, tok)], tok_sent, tpair_recv.at[2, 0], partner)
+
+    def landed(ref, sem):
+        remote(ref, ref, send_sem.at[0], sem, partner).wait_recv()
+
+    def left(ref, sem):
+        remote(ref, ref, sem, tpair_recv.at[0, 0], partner).wait_send()
 
     pl.semaphore_wait(barrier, 4)
     tok_out(1, 0).start()
     tok_out(2, 0).start()
-    for c in range(CHUNKS):
-        tok_pair(0, c).start()
+    own_pair.start()
 
     sub = lax.broadcasted_iota(jnp.int32, (64, tok), 0)
     chosen = jnp.zeros((64, tok), F32)
@@ -158,14 +169,16 @@
     want = jnp.where(half == own_half, want, -2.0)
 
     def masks(rels):
-        for rel in rels:
-            meta_pair(rel).wait_recv()
+        if rels == (0,):
+            meta_pair(0).wait_recv()
+        else:
+            landed(meta_all.at[pl.ds(1, 3), pl.ds(tok, tok)], mpair_recv.at[1])
         for rel in rels:
             meta = meta_all[rel]
             g1 = meta.astype(BF16)
-            left = meta - g1.astype(F32)
-            g2 = left.astype(BF16)
-            g3 = (left - g2.astype(F32)).astype(BF16)
+            rest = meta - g1.astype(F32)
+            g2 = rest.astype(BF16)
+            g3 = (rest - g2.astype(F32)).astype(BF16)
             rank_e = jnp.dot(g1, pick_rank, preferred_element_type=F32)
             hit = rank_e == want
             for i, g in enumerate((g1, g2, g3)):
@@ -180,14 +193,19 @@
             tok_pair(via, c).start()
 
     def diag_arrived(c):
-        for via in (1, 2):
-            tok_diag(via, c).wait_recv()
+        cols = pl.ds(c * chunk, chunk)
+        landed(x_all.at[3, pl.ds(0, tok), cols], diag_recv.at[c])
         tok_pair(3, c).start()
 
     def place(rels, cs):
         for c in cs:
-            for rel in rels:
-                tok_pair(rel, c).wait_recv()
+            cols = pl.ds(c * chunk, chunk)
+            if 0 in rels and c == 0:
+                own_pair.wait_recv()
+            if 1 in rels:
+                landed(x_all.at[pl.ds(1, 2), pl.ds(tok, tok), cols], tpair_recv.at[1, c])
+            if 3 in rels:
+                landed(x_all.at[3, pl.ds(tok, tok), cols], tpair_recv.at[0, c])
         for c in cs:
             for rel in rels:
                 rows = lax.dot_general(one_hot[rel], x_all[rel, :, c * chunk:(c + 1) * chunk],
@@ -208,8 +226,8 @@
         for e in range(EARLY):
             acc[e] = late_dot(e, 0, chunk)
 
-    def work_second():
-        for e in range(EARLY):
+    def work_second(e0, e1):
+        for e in range(e0, e1):
             acc[e] = acc[e] + late_dot(e, chunk, 2 * chunk)
 
     def work_third(e0, e1):
@@ -229,29 +247,31 @@
     masks((0,))
     place((0,), range(CHUNKS))
     early(0)
-    early(1)
     arrived(0)
     tok_out(1, 3).start()
     tok_out(2, 3).start()
-    early(2)
+    early(1)
     for rel in (1, 2, 3):
         meta_out(rel).wait_recv()
         meta_pair(rel).start()
     arrived(1)
-    early(3)
+    early(2)
     arrived(2)
     masks((1, 2, 3))
     diag_arrived(0)
-    place((1, 2), (0,))
+    early(3)
     arrived(3)
     diag_arrived(1)
+    place((1, 2), (0,))
     place((3,), (0,))
     work_first()
     diag_arrived(2)
+    place((1, 2, 3), (1,))
+    work_second(0, 2)
     diag_arrived(3)
-    place((1, 2, 3), (1,))
-    work_second()
-    place((1, 2, 3), (2, 3))
+    work_second(2, 4)
+    place((1, 2, 3), (2,))
+    place((1, 2, 3), (3,))
     work_third(0, 2)
     work_third(2, 4)
     down_start(1)
@@ -261,22 +281,22 @@
     down_start(3)
 
     def pair_copy(b):
-        return remote(part_send.at[b], part_recv.at[b], pair_send.at[b], pair_recv.at[b], partner)
+        return remote(part_send.at[b], part_recv.at[b], pair_sent, pair_recv.at[b], partner)
 
     lo, hi = pl.ds(0, HALF), pl.ds(HALF, HALF)
     everyone = pl.ds(0, 2)
 
     def first_x(b):
-        return remote(part_own.at[b, everyone, 1, :, lo], in_x1.at[b], red_send.at[b, 0], red_recv.at[b, 0], dev(1, False))
+        return remote(part_own.at[b, everyone, 1, :, lo], in_x1.at[b], one_sent, one_recv.at[b, 0], dev(1, False))
 
     def first_y(b):
-        return remote(part_own.at[b, 1, everyone, :, hi], in_y1.at[b], red_send.at[b, 1], red_recv.at[b, 1], dev(2, False))
+        return remote(part_own.at[b, 1, everyone, :, hi], in_y1.at[b], one_sent, one_recv.at[b, 1], dev(2, False))
 
     def second_y(b):
-        return remote(part_own.at[b, 1, 0, :, lo], in_y2.at[b], red_send.at[b, 2], red_recv.at[b, 2], dev(2, False))
+        return remote(part_own.at[b, 1, 0, :, lo], in_two.at[b, 0], two_sent, two_recv.at[b], dev(2, False))
 
     def second_x(b):
-        return remote(part_own.at[b, 0, 1, :, hi], in_x2.at[b], red_send.at[b, 3], red_recv.at[b, 3], dev(1, False))
+        return remote(part_own.at[b, 0, 1, :, hi], in_two.at[b, 1], two_sent, two_recv.at[b], dev(1, False))
 
     def stage_one(b):
         pair_copy(b).wait_recv()
@@ -312,11 +332,11 @@
         combine(0)
 
     def down_step(b, carry):
-        for e in range(n_exp):
-            down_copy(b, e).wait()
+        down_wait(b)
         for e in range(n_exp):
             slot, col = down_place(b, e)
             down_dot(e, up_buf[slot, 0:ff, col:col + COLS])
+        combine(b)
 
         @pl.when(b + RING < n_blk)
         def _():
@@ -327,29 +347,20 @@
         @pl.when(b > 2)
         def _():
             stage_two(b - 3)
-
-        combine(b)
         return carry
 
-    def out_copy(b):
-        cols = pl.ds(pl.multiple_of(b * COLS, COLS), COLS)
-        return pltpu.make_async_copy(out_v.at[b], out_hbm.at[:, cols], out_sem.at[b])
-
     def finish(b, carry):
-        second_y(b).wait_recv()
-        left = part_own[b, 0, 0, :, 0:HALF] + in_x1[b, 0] + in_y2[b]
-        out_v[b, :, 0:HALF] = left.astype(BF16)
-        second_x(b).wait_recv()
-        right = part_own[b, 0, 0, :, HALF:COLS] + in_y1[b, 0] + in_x2[b]
-        out_v[b, :, HALF:COLS] = right.astype(BF16)
-        out_copy(b).start()
+        landed(in_two.at[b], two_recv.at[b])
+        col = pl.multiple_of(b * COLS, COLS)
+        out_ref[:, pl.ds(col, HALF)] = (part_own[b, 0, 0, :, 0:HALF] + in_x1[b, 0] + in_two[b, 0]).astype(BF16)
+        out_ref[:, pl.ds(col + HALF, HALF)] = (part_own[b, 0, 0, :, HALF:COLS] + in_y1[b, 0] + in_two[b, 1]).astype(BF16)
         return carry
 
     last = n_blk - 1
 
     def last_copy(rel):
         return remote(part_own.at[last, rel // 2, rel % 2], in_last.at[rel - 1],
-                      last_send.at[rel - 1], last_recv.at[rel - 1], dev(rel, False))
+                      last_sent, last_recv.at[0], dev(rel, False))
 
     down_first()
     lax.fori_loop(1, n_blk, down_step, 0)
@@ -361,37 +372,16 @@
         last_copy(rel).start()
     stage_two(last - 1)
     lax.fori_loop(last - 4, last, finish, 0)
-    for rel in (1, 2, 3):
-        last_copy(rel).wait_recv()
+    landed(in_last, last_recv.at[0])
     total = part_own[last, 0, 0] + in_last[0] + in_last[1] + in_last[2]
-    out_v[last] = total.astype(BF16)
-    out_copy(last).start()
-
-    for rel in range(4):
-        meta_pair(rel).wait_send()
-        if rel:
-            meta_out(rel).wait_send()
-        for c in range(CHUNKS):
-            tok_pair(rel, c).wait_send()
-            if rel in (1, 2):
-                tok_out(rel, c).wait_send()
-                tok_diag(rel, c).wait_send()
-
-    for rel in (1, 2, 3):
-        last_copy(rel).wait_send()
-    pair_copy(last).wait_send()
-
-    def drain(b, carry):
-        for copy in (pair_copy, first_x, first_y, second_x, second_y):
-            copy(b).wait_send()
-        return carry
-
-    lax.fori_loop(0, last, drain, 0)
-    def flush(b, carry):
-        out_copy(b).wait()
-        return carry
-
-    lax.fori_loop(0, n_blk, flush, 0)
+    out_ref[:, last * COLS:] = total.astype(BF16)
+
+    left(slots.at[pl.ds(0, 7), pl.ds(0, tok)], tok_sent)
+    left(in_x1.at[pl.ds(0, 7), 0], meta_sent)
+    left(part_recv, pair_sent)
+    left(part_own.at[pl.ds(0, last), 0], one_sent)
+    left(in_x1.at[pl.ds(0, last)], two_sent)
+    left(in_last, last_sent)
 
 
 def solution(mesh):
@@ -412,13 +402,12 @@
         hbm = pl.BlockSpec(memory_space=pl.ANY)
         return pl.pallas_call(
             functools.partial(moe_kernel, dims),
-            out_shape=jax.ShapeDtypeStruct((tok, dim), BF16),
+            out_shape=pltpu.VMEM((tok, dim), BF16),
             in_specs=[hbm] * 5,
-            out_specs=hbm,
+            out_specs=pl.BlockSpec(memory_space=pltpu.VMEM),
             scratch_shapes=[
                 pltpu.VMEM((UP_SLOTS, dim, ff), BF16),
                 pltpu.VMEM((n_exp, ff, COLS), BF16),
-                pltpu.VMEM((n_blk, tok, COLS), BF16),
                 pltpu.VMEM((top_n, tok), jnp.int32),
                 pltpu.VMEM((top_n, tok), F32),
                 pltpu.VMEM((4, pair, dim), BF16),
@@ -434,18 +423,13 @@
                 pltpu.VMEM((n_blk, 2, 2, tok, COLS), F32),
                 pltpu.VMEM((n_blk, 2, tok, HALF), F32),
                 pltpu.VMEM((n_blk, 2, tok, HALF), F32),
-                pltpu.VMEM((n_blk, tok, HALF), F32),
-                pltpu.VMEM((n_blk, tok, HALF), F32),
+                pltpu.VMEM((n_blk, 2, tok, HALF), F32),
                 pltpu.VMEM((3, tok, COLS), F32),
-                dma((UP_SLOTS,)), dma((1,)), dma((RING, n_exp)), dma((n_blk,)), dma((3,)),
-                dma((4,)), dma((4,)),
-                dma((3, CHUNKS)), dma((3, CHUNKS)), dma((3, CHUNKS)), dma((3, CHUNKS)),
-                dma((4,)), dma((4,)), dma((4, CHUNKS)), dma((4, CHUNKS)),
-                dma((n_blk,)), dma((n_blk,)), dma((n_blk, 4)), dma((n_blk, 4)),
-                dma((3,)), dma((3,)),
+                dma((UP_SLOTS,)), dma((1,)), dma((RING,)), dma((3,)), dma((6,)), dma((3,)), dma((2,)),
+                dma((2, CHUNKS)), dma((CHUNKS,)), dma((3, CHUNKS)), dma((n_blk,)), dma((n_blk, 2)), dma((n_blk,)), dma((1,)),
             ],
             compiler_params=pltpu.CompilerParams(
-                collective_id=0, has_side_effects=True, vmem_limit_bytes=67043328),
+                collective_id=0, has_side_effects=True, vmem_limit_bytes=67043328 - 2 * tok * dim),
             name='moe_layer',
         )(x_loc, ids_loc.T, gates_loc.T, w_up, w_down)
 

time: 52.1 us -> 47.3 us (0.908)
  Pallas kernels: 50.3 us -> 46.5 us
  local copies, waits for them, and re-layouts: 1.62 us -> 0.68 us
    pallas_call x1, Pallas kernels: 50.3 us -> 46.5 us  [local_layer(): pl.pallas_call(functools.partial(moe_kernel, dims), out_shape=pltpu.VMEM(...]
    unnamed x1, local copies, waits for them, and re-layouts: 1.62 us -> 0.68 us
where the time goes in v3:
time: 47.3 us; the launch traced here: 47.2 us
  Pallas kernels  46.5 us (98%)
  local copies, waits for them, and re-layouts  0.68 us (1%)
    pallas_call x1, Pallas kernels, local_layer(): pl.pallas_call(functools.partial(moe_kernel, dims), out_shape=pltpu.VMEM(...  46.5 us

profile of v3, /device:TPU:0, one launch (start us, length us, event | category | flops | bytes accessed | tf_op | source)
XLA Modules:
  0.0 47.2 jit_solution(14331109019842855062)
XLA Ops:
  0.0 46.5 %moe_layer.1 = bf16[48,2048]{1,0:T(8,128)(2,1)S(1)} custom-call(bf16[48,2048]{1,0:T(8,128)(2,1)} %x_hbm.1, s32[6,48]{1,0:T(8,128)} %bitcast.2, f32[6,48]{1,0:T(8,128)} %bitcast.3, bf16[8,2048,1408]{2,1,0:T(8,128)(2,1)} %up_hbm.1, bf16[8,1408,2048]{2,1,0:T(8,128)(2,1)} %down_hbm.1), custom_call_target="tpu_custom_call" | custom-call | tf_op jit(solution)/shard_map/moe_layer/pallas_call | solution.py:403
  46.5 0.7 %copy.7 = bf16[48,2048]{1,0:T(8,128)(2,1)} copy(bf16[48,2048]{1,0:T(8,128)(2,1)S(1)} %moe_layer.1) | data formatting | bytes 393216

commit v4 on v3

--- a/solution.py
+++ b/solution.py
@@ -29,7 +29,7 @@
                up_buf, first_buf, ids_v, gates_v, x_all, meta_all, one_hot, slots, acc, hidden, mix, expert_out,
                part_own, part_send, part_recv, in_x1, in_y1, in_two, in_last,
                up_sem, first_sem, down_sem, in_sem, send_sem, meta_recv, mpair_recv,
-               tok_recv, diag_recv, tpair_recv, pair_recv, one_recv, two_recv, last_recv):
+               tok_recv, diag_recv, tpair_recv, pair_recv, near_recv, one_recv, two_recv, last_recv, own_recv):
     tok, top_n, dim, ff, n_exp, cap = dims
     pair = 2 * tok
     per_exp = 2 * cap
@@ -109,7 +109,7 @@
     def tok_out(rel, c):
         cols = pl.ds(c * chunk, chunk)
         return remote(x_all.at[0, pl.ds(0, tok), cols], x_all.at[rel, pl.ds(0, tok), cols],
-                      tok_sent, tok_recv.at[rel - 1, c], dev(rel, False))
+                      tok_sent, tok_recv.at[c], dev(rel, False))
 
     def tok_diag(via, c):
         cols = pl.ds(c * chunk + (via - 1) * (chunk // 2), chunk // 2)
@@ -121,7 +121,7 @@
         return remote(x_all.at[rel, pl.ds(0, tok), cols], x_all.at[rel, pl.ds(tok, tok), cols],
                       tok_sent, tpair_recv.at[0 if rel == 3 else 1, c], partner)
 
-    own_pair = remote(x_all.at[0, pl.ds(0, tok)], x_all.at[0, pl.ds(tok, tok)], tok_sent, tpair_recv.at[2, 0], partner)
+    own_pair = remote(x_all.at[0, pl.ds(0, tok)], x_all.at[0, pl.ds(tok, tok)], tok_sent, own_recv.at[0], partner)
 
     def landed(ref, sem):
         remote(ref, ref, send_sem.at[0], sem, partner).wait_recv()
@@ -187,8 +187,8 @@
             one_hot[rel] = jnp.where(hit, 1.0, 0.0).astype(BF16)
 
     def arrived(c):
+        landed(x_all.at[pl.ds(1, 2), pl.ds(0, tok), pl.ds(c * chunk, chunk)], tok_recv.at[c])
         for via in (1, 2):
-            tok_out(via, c).wait_recv()
             tok_diag(via, c).start()
             tok_pair(via, c).start()
 
@@ -258,12 +258,12 @@
     early(2)
     arrived(2)
     masks((1, 2, 3))
+    place((1, 2), (0,))
     diag_arrived(0)
+    arrived(3)
     early(3)
-    arrived(3)
+    place((3,), (0,))
     diag_arrived(1)
-    place((1, 2), (0,))
-    place((3,), (0,))
     work_first()
     diag_arrived(2)
     place((1, 2, 3), (1,))
@@ -312,69 +312,117 @@
         part_own[b, 0, 1, :, HALF:COLS] = part_own[b, 0, 1, :, HALF:COLS] + in_y1[b, 1]
         second_x(b).start()
 
-    def down_dot(e, weights):
-        o = jnp.dot(hidden[e], weights, preferred_element_type=F32).astype(BF16)
-        for rel in range(4):
-            expert_out[rel, e * per_exp:(e + 1) * per_exp, :] = o[rel * per_exp:(rel + 1) * per_exp]
-
-    def combine(b):
-        for rel in range(4):
+    def down_dot(e, weights, rels):
+        first, count = rels[0] * per_exp, len(rels) * per_exp
+        o = jnp.dot(hidden[e, first:first + count, :], weights, preferred_element_type=F32).astype(BF16)
+        for i, rel in enumerate(rels):
+            expert_out[rel, e * per_exp:(e + 1) * per_exp, :] = o[i * per_exp:(i + 1) * per_exp]
+
+    def down_dots(b, rels):
+        for e in range(n_exp):
+            slot, col = down_place(b, e)
+            down_dot(e, up_buf[slot, 0:ff, col:col + COLS], rels)
+
+    def combine(b, rels):
+        for rel in rels:
             y3 = jnp.dot(mix[rel], expert_out[rel], preferred_element_type=F32)
             y = y3[0:pair] + (y3[pair:2 * pair] + y3[2 * pair:3 * pair])
             part_own[b, rel // 2, rel % 2] = y[0:tok]
             part_send[b, rel // 2, rel % 2] = y[tok:pair]
-        pair_copy(b).start()
-
-    def down_first():
-        first_copy.wait()
-        for e in range(n_exp):
-            down_dot(e, first_buf[e])
-        combine(0)
+
+    every, far, near = (0, 1, 2, 3), (1, 2, 3), (0,)
 
     def down_step(b, carry):
         down_wait(b)
-        for e in range(n_exp):
-            slot, col = down_place(b, e)
-            down_dot(e, up_buf[slot, 0:ff, col:col + COLS])
-        combine(b)
-
-        @pl.when(b + RING < n_blk)
-        def _():
-            down_start(b + RING)
-
+        down_dots(b, every)
+        combine(b, every)
+        pair_copy(b).start()
         stage_one(b - 1)
 
         @pl.when(b > 2)
         def _():
             stage_two(b - 3)
+
+        down_start(b + RING)
         return carry
+
+    def far_part(b, i):
+        where = (b, 0, 1) if i == 0 else (b, 1)
+        return remote(part_send.at[where], part_recv.at[where], pair_sent, pair_recv.at[b], partner)
+
+    def near_part(b):
+        return remote(part_send.at[b, 0, 0], part_recv.at[b, 0, 0], pair_sent, near_recv.at[b - split], partner)
+
+    def work_far(b):
+        down_wait(b)
+        down_dots(b, far)
+        combine(b, far)
+        far_part(b, 0).start()
+        far_part(b, 1).start()
+
+    def work_near(b):
+        down_dots(b, near)
+        combine(b, near)
+        near_part(b).start()
+
+    def add_far(b):
+        landed(in_last, pair_recv.at[b])
+        part_own[b, 0, 1] = part_own[b, 0, 1] + part_recv[b, 0, 1]
+        part_own[b, 1] = part_own[b, 1] + part_recv[b, 1]
+
+    def stage_far(b):
+        add_far(b)
+        first_x(b).start()
+        first_y(b).start()
 
     def finish(b, carry):
         landed(in_two.at[b], two_recv.at[b])
-        col = pl.multiple_of(b * COLS, COLS)
-        out_ref[:, pl.ds(col, HALF)] = (part_own[b, 0, 0, :, 0:HALF] + in_x1[b, 0] + in_two[b, 0]).astype(BF16)
-        out_ref[:, pl.ds(col + HALF, HALF)] = (part_own[b, 0, 0, :, HALF:COLS] + in_y1[b, 0] + in_two[b, 1]).astype(BF16)
+        own = part_own[b, 0, 0]
+        if not isinstance(b, jax.Array):
+            near_part(b).wait_recv()
+            own = own + part_recv[b, 0, 0]
+        col = b * COLS if not isinstance(b, jax.Array) else pl.multiple_of(b * COLS, COLS)
+        out_ref[:, pl.ds(col, HALF)] = (own[:, 0:HALF] + in_x1[b, 0] + in_two[b, 0]).astype(BF16)
+        out_ref[:, pl.ds(col + HALF, HALF)] = (own[:, HALF:COLS] + in_y1[b, 0] + in_two[b, 1]).astype(BF16)
         return carry
 
     last = n_blk - 1
+    split = n_blk - RING
 
     def last_copy(rel):
         return remote(part_own.at[last, rel // 2, rel % 2], in_last.at[rel - 1],
                       last_sent, last_recv.at[0], dev(rel, False))
 
-    down_first()
-    lax.fori_loop(1, n_blk, down_step, 0)
-    stage_two(last - 2)
-    lax.fori_loop(0, last - 4, finish, 0)
-    pair_copy(last).wait_recv()
-    part_own[last] = part_own[last] + part_recv[last]
+    first_copy.wait()
+    for e in range(n_exp):
+        down_dot(e, first_buf[e], every)
+    combine(0, every)
+    pair_copy(0).start()
+    lax.fori_loop(1, split, down_step, 0)
+    work_far(split)
+    stage_one(split - 1)
+    stage_two(split - 3)
+    work_far(split + 1)
+    stage_far(split)
+    stage_two(split - 2)
+    work_far(split + 2)
+    stage_far(split + 1)
+    work_near(split)
+    stage_two(split - 1)
+    add_far(last)
     for rel in (3, 1, 2):
         last_copy(rel).start()
-    stage_two(last - 1)
-    lax.fori_loop(last - 4, last, finish, 0)
+    work_near(split + 1)
+    stage_two(split)
+    work_near(split + 2)
+    stage_two(split + 1)
+    lax.fori_loop(0, split, finish, 0)
+    finish(split, 0)
+    finish(split + 1, 0)
+    near_part(last).wait_recv()
+    own_last = part_own[last, 0, 0] + part_recv[last, 0, 0]
     landed(in_last, last_recv.at[0])
-    total = part_own[last, 0, 0] + in_last[0] + in_last[1] + in_last[2]
-    out_ref[:, last * COLS:] = total.astype(BF16)
+    out_ref[:, last * COLS:] = (own_last + in_last[0] + in_last[1] + in_last[2]).astype(BF16)
 
     left(slots.at[pl.ds(0, 7), pl.ds(0, tok)], tok_sent)
     left(in_x1.at[pl.ds(0, 7), 0], meta_sent)
@@ -426,7 +474,7 @@
                 pltpu.VMEM((n_blk, 2, tok, HALF), F32),
                 pltpu.VMEM((3, tok, COLS), F32),
                 dma((UP_SLOTS,)), dma((1,)), dma((RING,)), dma((3,)), dma((6,)), dma((3,)), dma((2,)),
-                dma((2, CHUNKS)), dma((CHUNKS,)), dma((3, CHUNKS)), dma((n_blk,)), dma((n_blk, 2)), dma((n_blk,)), dma((1,)),
+                dma((CHUNKS,)), dma((CHUNKS,)), dma((2, CHUNKS)), dma((n_blk,)), dma((RING,)), dma((n_blk - 1, 2)), dma((n_blk - 1,)), dma((1,)), dma((1,)),
             ],
             compiler_params=pltpu.CompilerParams(
                 collective_id=0, has_side_effects=True, vmem_limit_bytes=67043328 - 2 * tok * dim),

time: 47.3 us -> 46.7 us (0.987)
  Pallas kernels: 46.5 us -> 45.9 us
    pallas_call x1, Pallas kernels: 46.5 us -> 45.9 us  [local_layer(): pl.pallas_call(functools.partial(moe_kernel, dims), out_shape=pltpu.VMEM(...]
where the time goes in v4:
time: 46.7 us; the launch traced here: 46.6 us
  Pallas kernels  45.9 us (98%)
  local copies, waits for them, and re-layouts  0.68 us (1%)
    pallas_call x1, Pallas kernels, local_layer(): pl.pallas_call(functools.partial(moe_kernel, dims), out_shape=pltpu.VMEM(...  45.9 us

profile of v4, /device:TPU:0, one launch (start us, length us, event | category | flops | bytes accessed | tf_op | source)
XLA Modules:
  0.0 46.6 jit_solution(9796607088018742283)
XLA Ops:
  0.0 45.9 %moe_layer.1 = bf16[48,2048]{1,0:T(8,128)(2,1)S(1)} custom-call(bf16[48,2048]{1,0:T(8,128)(2,1)} %x_hbm.1, s32[6,48]{1,0:T(8,128)} %bitcast.2, f32[6,48]{1,0:T(8,128)} %bitcast.3, bf16[8,2048,1408]{2,1,0:T(8,128)(2,1)} %up_hbm.1, bf16[8,1408,2048]{2,1,0:T(8,128)(2,1)} %down_hbm.1), custom_call_target="tpu_custom_call" | custom-call | tf_op jit(solution)/shard_map/moe_layer/pallas_call | solution.py:451
  45.9 0.7 %copy.7 = bf16[48,2048]{1,0:T(8,128)(2,1)} copy(bf16[48,2048]{1,0:T(8,128)(2,1)S(1)} %moe_layer.1) | data formatting | bytes 393216

commit v5 on v4

--- a/solution.py
+++ b/solution.py
@@ -287,10 +287,10 @@
     everyone = pl.ds(0, 2)
 
     def first_x(b):
-        return remote(part_own.at[b, everyone, 1, :, lo], in_x1.at[b], one_sent, one_recv.at[b, 0], dev(1, False))
+        return remote(part_own.at[b, everyone, 1, :, lo], in_x1.at[b], one_sent, one_recv.at[b], dev(1, False))
 
     def first_y(b):
-        return remote(part_own.at[b, 1, everyone, :, hi], in_y1.at[b], one_sent, one_recv.at[b, 1], dev(2, False))
+        return remote(part_own.at[b, 1, everyone, :, hi], in_y1.at[b], one_sent, one_recv.at[b], dev(2, False))
 
     def second_y(b):
         return remote(part_own.at[b, 1, 0, :, lo], in_two.at[b, 0], two_sent, two_recv.at[b], dev(2, False))
@@ -305,10 +305,9 @@
         first_y(b).start()
 
     def stage_two(b):
-        first_x(b).wait_recv()
+        landed(in_x1.at[pl.ds(0, 2)], one_recv.at[b])
         part_own[b, 1, 0, :, 0:HALF] = part_own[b, 1, 0, :, 0:HALF] + in_x1[b, 1]
         second_y(b).start()
-        first_y(b).wait_recv()
         part_own[b, 0, 1, :, HALF:COLS] = part_own[b, 0, 1, :, HALF:COLS] + in_y1[b, 1]
         second_x(b).start()
 
@@ -474,7 +473,7 @@
                 pltpu.VMEM((n_blk, 2, tok, HALF), F32),
                 pltpu.VMEM((3, tok, COLS), F32),
                 dma((UP_SLOTS,)), dma((1,)), dma((RING,)), dma((3,)), dma((6,)), dma((3,)), dma((2,)),
-                dma((CHUNKS,)), dma((CHUNKS,)), dma((2, CHUNKS)), dma((n_blk,)), dma((RING,)), dma((n_blk - 1, 2)), dma((n_blk - 1,)), dma((1,)), dma((1,)),
+                dma((CHUNKS,)), dma((CHUNKS,)), dma((2, CHUNKS)), dma((n_blk,)), dma((RING,)), dma((n_blk - 1,)), dma((n_blk - 1,)), dma((1,)), dma((1,)),
             ],
             compiler_params=pltpu.CompilerParams(
                 collective_id=0, has_side_effects=True, vmem_limit_bytes=67043328 - 2 * tok * dim),

time: 46.7 us -> 46.7 us (level)
  no operation moved by 1% of the time
where the time goes in v5:
time: 46.7 us; the launch traced here: 46.6 us
  Pallas kernels  45.9 us (98%)
  local copies, waits for them, and re-layouts  0.68 us (1%)
    pallas_call x1, Pallas kernels, local_layer(): pl.pallas_call(functools.partial(moe_kernel, dims), out_shape=pltpu.VMEM(...  45.9 us

profile of v5, /device:TPU:0, one launch (start us, length us, event | category | flops | bytes accessed | tf_op | source)
XLA Modules:
  0.0 46.6 jit_solution(16952755724795141789)
XLA Ops:
  0.0 45.9 %moe_layer.1 = bf16[48,2048]{1,0:T(8,128)(2,1)S(1)} custom-call(bf16[48,2048]{1,0:T(8,128)(2,1)} %x_hbm.1, s32[6,48]{1,0:T(8,128)} %bitcast.2, f32[6,48]{1,0:T(8,128)} %bitcast.3, bf16[8,2048,1408]{2,1,0:T(8,128)(2,1)} %up_hbm.1, bf16[8,1408,2048]{2,1,0:T(8,128)(2,1)} %down_hbm.1), custom_call_target="tpu_custom_call" | custom-call | tf_op jit(solution)/shard_map/moe_layer/pallas_call | solution.py:450
  45.9 0.7 %copy.7 = bf16[48,2048]{1,0:T(8,128)(2,1)} copy(bf16[48,2048]{1,0:T(8,128)(2,1)S(1)} %moe_layer.1) | data formatting | bytes 393216
